TPU v7x, 32 devices: a whole 2x2x4 slice. The times are simulated.
32 devices in a mesh: mod: 4 (over x, core), shard: 8 (over z, y).
Axes of the slice: x: 2, y: 2, z: 4, core: 2. Of those that a mesh axis runs over, the one named last changes fastest.
Arguments:
- tokens_b: bfloat16 [512, 4096], P(('mod', 'shard')), may hold values from -6 to 6
- labels_b: int32 [512, 1], P(('mod', 'shard')), may hold values from 0 to 3; in each aligned block of 16 rows (0 to 15, 16 to 31, ...) at most 6 rows name the same one
- tokens_a: bfloat16 [512, 4096], P(('mod', 'shard')), may hold values from -6 to 6
- labels_a: int32 [512, 1], P(('mod', 'shard')), may hold values from 0 to 3; in each aligned block of 16 rows (0 to 15, 16 to 31, ...) at most 6 rows name the same one
- grad_out_a: bfloat16 [512, 4096], P(('mod', 'shard')), may hold values from -6 to 6
- gate_saved: bfloat16 [4, 192, 11008], P('mod', None, 'shard'), may hold values from -6 to 6
- up_saved: bfloat16 [4, 192, 11008], P('mod', None, 'shard'), may hold values from -6 to 6
- gate_weight: bfloat16 [4, 4096, 11008], P('mod', None, 'shard'), may hold values from -0.09375 to 0.09375
- up_weight: bfloat16 [4, 4096, 11008], P('mod', None, 'shard'), may hold values from -0.09375 to 0.09375
- down_weight: bfloat16 [4, 11008, 4096], P('mod', 'shard'), may hold values from -0.0546875 to 0.0546875
Outputs:
- output_b: bfloat16 [512, 4096], P(('mod', 'shard'))
- grad_tokens_a: bfloat16 [512, 4096], P(('mod', 'shard'))
- grad_gate: bfloat16 [4, 4096, 11008], P('mod', None, 'shard')
- grad_up: bfloat16 [4, 4096, 11008], P('mod', None, 'shard')
- grad_down: bfloat16 [4, 11008, 4096], P('mod', 'shard')
Inputs may be any that keep to these rules, and one draw needn't show every extreme that they name: `labels_b`: among the 16 tokens of one home device no label occurs more than 6 times; in every draw some home device has exactly 6 tokens of one label. `labels_a`: among the 16 tokens of one home device no label occurs more than 6 times; in every draw some home device has exactly 6 tokens of one label.
All inputs are finite; a program needn't handle non-finite values.
Results may differ from a plain program's by a relative error of at most 0.0049.
Values may be sent and summed in bfloat16 or wider, within the bound.
A program may use at most 128 MiB of HBM per device.

v0:
```python
import jax
import jax.numpy as jnp
from jax import lax
from jax.sharding import PartitionSpec as P

CAP = 6


def place_table(labels, modes):
    lab = labels[:, 0]
    onehot = (lab[:, None] == jnp.arange(modes, dtype=jnp.int32)[None, :]).astype(jnp.int32)
    rank = jnp.cumsum(onehot, axis=0) - onehot
    slot = jnp.sum(rank * onehot, axis=1)
    within = (slot[:, None] == jnp.arange(CAP, dtype=jnp.int32)[None, :]).astype(jnp.int32)
    table = onehot[:, :, None] * within[:, None, :]
    return table.reshape(lab.shape[0], modes * CAP).astype(jnp.bfloat16)


def dispatch(place, values, modes):
    sent = lax.dot_general(
        place, values, (((0,), (0,)), ((), ())), preferred_element_type=jnp.float32
    )
    return sent.astype(jnp.bfloat16).reshape(modes, CAP, values.shape[1])


def collect(place, arrived):
    flat = arrived.reshape(place.shape[1], arrived.shape[2])
    return jnp.dot(place, flat, preferred_element_type=jnp.float32).astype(jnp.bfloat16)


def contract_last(left, right):
    return lax.dot_general(
        left, right, (((1,), (1,)), ((), ())), preferred_element_type=jnp.float32
    )


def forward_pass(tokens_b, labels_b, gate_w, up_w, down_w):
    modes = lax.axis_size("mod")
    width = tokens_b.shape[1]
    place = place_table(labels_b, modes)
    sent = dispatch(place, tokens_b, modes)
    arrived = lax.all_to_all(sent, "mod", split_axis=0, concat_axis=0, tiled=True)
    local_rows = arrived.reshape(modes * CAP, width)
    piece = lax.all_gather(local_rows, "shard", axis=0, tiled=True)
    gate = jnp.dot(piece, gate_w, preferred_element_type=jnp.float32)
    up = jnp.dot(piece, up_w, preferred_element_type=jnp.float32)
    terms = jnp.dot(
        (jax.nn.silu(gate) * up).astype(jnp.bfloat16), down_w, preferred_element_type=jnp.float32
    )
    summed = lax.psum_scatter(terms, "shard", scatter_dimension=0, tiled=True)
    back = summed.astype(jnp.bfloat16).reshape(modes, CAP, width)
    returned = lax.all_to_all(back, "mod", split_axis=0, concat_axis=0, tiled=True)
    return collect(place, returned)


def backward_pass(tokens_a, labels_a, grad_out_a, gate_s, up_s, gate_w, up_w, down_w):
    modes = lax.axis_size("mod")
    width = tokens_a.shape[1]
    place = place_table(labels_a, modes)
    sent_x = dispatch(place, tokens_a, modes)
    sent_g = dispatch(place, grad_out_a, modes)
    arrived_x, arrived_g = (
        lax.all_to_all(sent_x, "mod", split_axis=0, concat_axis=0, tiled=True),
        lax.all_to_all(sent_g, "mod", split_axis=0, concat_axis=0, tiled=True),
    )
    all_x, all_g = (
        lax.all_gather(arrived_x.reshape(modes * CAP, width), "shard", axis=0, tiled=True),
        lax.all_gather(arrived_g.reshape(modes * CAP, width), "shard", axis=0, tiled=True),
    )
    gate = gate_s.astype(jnp.float32)
    up = up_s.astype(jnp.float32)
    sig = jax.nn.sigmoid(gate)
    act = gate * sig
    dh = contract_last(all_g, down_w)
    dgate = (dh * up * sig * (1.0 + gate * (1.0 - sig))).astype(jnp.bfloat16)
    dup = (dh * act).astype(jnp.bfloat16)
    hidden = (act * up).astype(jnp.bfloat16)
    outer = (((0,), (0,)), ((), ()))
    grad_down = lax.dot_general(hidden, all_g, outer, preferred_element_type=jnp.float32).astype(
        jnp.bfloat16
    )
    grad_gate = lax.dot_general(all_x, dgate, outer, preferred_element_type=jnp.float32).astype(
        jnp.bfloat16
    )
    grad_up = lax.dot_general(all_x, dup, outer, preferred_element_type=jnp.float32).astype(
        jnp.bfloat16
    )
    terms = contract_last(dgate, gate_w) + contract_last(dup, up_w)
    summed = lax.psum_scatter(terms, "shard", scatter_dimension=0, tiled=True)
    back = summed.astype(jnp.bfloat16).reshape(modes, CAP, width)
    returned = lax.all_to_all(back, "mod", split_axis=0, concat_axis=0, tiled=True)
    return (collect(place, returned), grad_gate[None], grad_up[None], grad_down[None])


def body(
    tokens_b,
    labels_b,
    tokens_a,
    labels_a,
    grad_out_a,
    gate_saved,
    up_saved,
    gate_weight,
    up_weight,
    down_weight,
):
    gate_w = gate_weight[0]
    up_w = up_weight[0]
    down_w = down_weight[0]
    output_b = forward_pass(tokens_b, labels_b, gate_w, up_w, down_w)
    grads = backward_pass(
        tokens_a, labels_a, grad_out_a, gate_saved[0], up_saved[0], gate_w, up_w, down_w
    )
    return (output_b, grads[0], grads[1], grads[2], grads[3])


def solution(mesh):
    return jax.shard_map(
        body,
        mesh=mesh,
        in_specs=(
            P(("mod", "shard"), None),
            P(("mod", "shard"), None),
            P(("mod", "shard"), None),
            P(("mod", "shard"), None),
            P(("mod", "shard"), None),
            P("mod", None, "shard"),
            P("mod", None, "shard"),
            P("mod", None, "shard"),
            P("mod", None, "shard"),
            P("mod", "shard", None),
        ),
        out_specs=(
            P(("mod", "shard"), None),
            P(("mod", "shard"), None),
            P("mod", None, "shard"),
            P("mod", None, "shard"),
            P("mod", "shard", None),
        ),
        check_vma=False,
    )
```

profile of v0, /device:TPU:0, one launch (start us, length us, event | category | flops | bytes accessed | tf_op | source)
XLA Modules:
  0.0 327.6 jit_solution(9912826482816697624)
XLA Ops:
  7.2 0.0 all-gather.6.cloned.1.call-start
  7.2 0.8 fusion.44
  8.0 0.1 copy.18
  8.2 0.8 select_reduce_fusion
  9.0 0.2 convolution_convert_fusion.4
  9.2 0.1 reshape.137
  9.3 10.2 %all_to_all.25 = bf16[4,6,4096]{2,1,0:T(8,128)(2,1)S(1)} all-to-all(bf16[4,6,4096]{2,1,0:T(8,128)(2,1)S(1)} %reshape.137), channel_id=1, replica_groups=mesh['mod'=4,'shard'=8] {'mod'}, dimensions={0} | all-to-all | bytes 393216 | tf_op jit(solution)/shard_map/all_to_all | solution.py:64
  19.5 0.7 reshape.138
  20.3 0.0 all-gather.4.cloned.1.call-start
  20.3 0.1 fusion.45
  20.4 0.1 copy.17
  20.5 0.2 select_reduce_fusion.1
  20.8 0.2 convolution_convert_fusion.5
  20.9 0.1 reshape.134
  21.1 8.5 %all_to_all.26 = bf16[4,6,4096]{2,1,0:T(8,128)(2,1)S(1)} all-to-all(bf16[4,6,4096]{2,1,0:T(8,128)(2,1)S(1)} %reshape.134), channel_id=1, replica_groups=mesh['mod'=4,'shard'=8] {'mod'}, dimensions={0} | all-to-all | bytes 393216 | tf_op jit(solution)/shard_map/all_to_all | solution.py:42
  29.6 0.7 reshape.135
  30.3 0.0 all-gather.4.cloned.1.call-update
  30.4 0.0 all-gather.8.cloned.1.call-start
  30.4 0.2 convolution_convert_fusion.3
  30.6 0.1 reshape.140
  30.7 8.4 %all_to_all.27 = bf16[4,6,4096]{2,1,0:T(8,128)(2,1)S(1)} all-to-all(bf16[4,6,4096]{2,1,0:T(8,128)(2,1)S(1)} %reshape.140), channel_id=1, replica_groups=mesh['mod'=4,'shard'=8] {'mod'}, dimensions={0} | all-to-all | bytes 393216 | tf_op jit(solution)/shard_map/all_to_all | solution.py:63
  39.1 0.8 reshape.141
  39.8 0.0 all-gather.8.cloned.1.call-update
  39.9 0.0 reduce-scatter.5.cloned.1.call-start
  39.9 25.0 %all-gather.6.cloned.1.call-done = bf16[192,4096]{1,0:T(8,128)(2,1)} async-done(((bf16[24,4096]{1,0:T(8,128)(2,1)}), bf16[192,4096]{1,0:T(8,128)(2,1)}) %all-gather.6.cloned.1.call-update) | async-done | bytes 1572880 | tf_op jit(solution)/shard_map/all_gather | solution.py:68
  64.9 8.9 %fusion.30 = (bf16[192,1376]{1,0:T(8,128)(2,1)S(1)}, f32[192,1376]{1,0:T(8,128)S(1)}) fusion(bf16[1,192,1376]{2,1,0:T(8,128)(2,1)S(1)} %copy-done.8, bf16[1,192,1376]{2,1,0:T(8,128)(2,1)S(1)} %copy-done.9, bf16[192,4096]{1,0:T(8,128)(2,1)} %all-gather.6.cloned.1.call-done, bf16[1,1376,4096]{2,1,0:T(8,128)(2,1)} %param.19), kind=kOutput, calls=%fused_computation.35 | convolution fusion | flops 2167431168 | bytes 15486976 | tf_op jit(solution)/shard_map/dot_general | solution.py:32
  73.9 6.2 %fusion.7 = f32[192,4096]{1,0:T(8,128)S(1)} fusion(bf16[1,4096,1376]{1,2,0:T(8,128)(2,1)} %param.18, f32[192,1376]{1,0:T(8,128)S(1)} %get-tuple-element.6, bf16[1,192,1376]{2,1,0:T(8,128)(2,1)S(1)} %copy-done.9), kind=kOutput, calls=%fused_computation.10 | convolution fusion | flops 2166110208 | bytes 16003072 | tf_op jit(solution)/shard_map/dot_general | solution.py:32
  80.1 4.5 %fusion.15 = f32[192,4096]{1,0:T(8,128)} fusion(f32[192,4096]{1,0:T(8,128)S(1)} %fusion.7, bf16[192,1376]{1,0:T(8,128)(2,1)S(1)} %get-tuple-element.5, bf16[1,4096,1376]{1,2,0:T(8,128)(2,1)S(1)} %bitcast.80), kind=kOutput, calls=%fused_computation.18 | convolution fusion | flops 2165047296 | bytes 18092032 | tf_op jit(solution)/shard_map/dot_general | solution.py:32
  84.6 0.2 reduce-scatter.3.cloned.1.call-start
  84.9 25.5 %all-gather.4.cloned.1.call-done = bf16[192,4096]{1,0:T(8,128)(2,1)} async-done(((bf16[24,4096]{1,0:T(8,128)(2,1)}), bf16[192,4096]{1,0:T(8,128)(2,1)}) %all-gather.4.cloned.1.call-update) | async-done | bytes 1572880 | tf_op jit(solution)/shard_map/all_gather | solution.py:44
  110.3 9.7 %fusion.13 = f32[192,1376]{1,0:T(8,128)} fusion(bf16[192,4096]{1,0:T(8,128)(2,1)} %all-gather.4.cloned.1.call-done, bf16[1,4096,1376]{1,2,0:T(8,128)(2,1)} %param.17), kind=kOutput, calls=%fused_computation.16 | convolution fusion | flops 2164260864 | bytes 13901824 | tf_op jit(solution)/shard_map/dot_general | solution.py:45
  120.0 15.8 %fusion.5 = f32[192,4096]{1,0:T(8,128)} fusion(bf16[1,1376,4096]{2,1,0:T(8,128)(2,1)} %param.19, bf16[192,4096]{1,0:T(8,128)(2,1)S(1)} %copy-done.7, bf16[1,4096,1376]{1,2,0:T(8,128)(2,1)} %param.18, f32[192,1376]{1,0:T(8,128)} %fusion.13), kind=kOutput, calls=%fused_computation.8 | convolution fusion | flops 4330106880 | bytes 28319744 | tf_op jit(solution)/shard_map/dot_general | solution.py:47
  135.9 1.5 copy-done.6
  137.4 7.1 %fusion = bf16[1,1376,4096]{2,1,0:T(8,128)(2,1)} fusion(bf16[192,4096]{1,0:T(8,128)(2,1)S(1)} %copy-done.6, bf16[1,192,1376]{2,1,0:T(8,128)(2,1)S(1)} %copy-done.8, bf16[1,192,1376]{2,1,0:T(8,128)(2,1)} %param.15), kind=kOutput, calls=%fused_computation.3 | convolution fusion | flops 2172010496 | bytes 13901824 | tf_op jit(solution)/shard_map/dot_general | solution.py:79
  144.6 10.6 %all-gather.8.cloned.1.call-done = bf16[192,4096]{1,0:T(8,128)(2,1)} async-done(((bf16[24,4096]{1,0:T(8,128)(2,1)}), bf16[192,4096]{1,0:T(8,128)(2,1)}) %all-gather.8.cloned.1.call-update) | async-done | bytes 1572880 | tf_op jit(solution)/shard_map/all_gather | solution.py:67
  155.1 9.5 %fusion.2 = bf16[1,4096,1376]{1,2,0:T(8,128)(2,1)} fusion(bf16[192,4096]{1,0:T(8,128)(2,1)} %all-gather.8.cloned.1.call-done, f32[192,1376]{1,0:T(8,128)} %copy-done.10, bf16[1,192,1376]{2,1,0:T(8,128)(2,1)} %param.15), kind=kOutput, calls=%fused_computation.5 | convolution fusion | flops 2171746304 | bytes 14430208 | tf_op jit(solution)/shard_map/dot_general | solution.py:85
  164.6 67.3 %reduce-scatter.5.cloned.1.call-done = f32[24,4096]{1,0:T(8,128)} async-done(((f32[192,4096]{1,0:T(8,128)}), f32[24,4096]{1,0:T(8,128)}) %reduce-scatter.5.cloned.1.call-update) | async-done | bytes 393232 | tf_op jit(solution)/shard_map/reduce_scatter | solution.py:89
  231.9 1.0 convert_element_type.115
  232.9 0.8 reshape.139
  233.7 3.4 %all-to-all-start.3 = ((bf16[4,6,4096]{2,1,0:T(8,128)(2,1)}), bf16[4,6,4096]{2,1,0:T(8,128)(2,1)S(1)}, u32[]{:S(2)}, u32[]{:S(2)}) async-start(bf16[4,6,4096]{2,1,0:T(8,128)(2,1)} %reshape.139), calls=%async_computation.5 | async-start | bytes 524288 | tf_op jit(solution)/shard_map/all_to_all | solution.py:91
  237.1 6.0 %fusion.1 = bf16[1,4096,1376]{1,2,0:T(8,128)(2,1)} fusion(bf16[192,4096]{1,0:T(8,128)(2,1)S(1)} %copy-done.2, bf16[192,1376]{1,0:T(8,128)(2,1)S(1)} %get-tuple-element.5), kind=kOutput, calls=%fused_computation.4 | convolution fusion | flops 2169896960 | bytes 13373440 | tf_op jit(solution)/shard_map/dot_general | solution.py:82
  243.2 65.8 %reduce-scatter.3.cloned.1.call-done = f32[24,4096]{1,0:T(8,128)} async-done(((f32[192,4096]{1,0:T(8,128)}), f32[24,4096]{1,0:T(8,128)}) %reduce-scatter.3.cloned.1.call-update) | async-done | bytes 393232 | tf_op jit(solution)/shard_map/reduce_scatter | solution.py:50
  309.0 1.0 convert_element_type.102
  310.0 0.8 reshape.136
  310.8 3.4 %all-to-all-start.1 = ((bf16[4,6,4096]{2,1,0:T(8,128)(2,1)}), bf16[4,6,4096]{2,1,0:T(8,128)(2,1)S(1)}, u32[]{:S(2)}, u32[]{:S(2)}) async-start(bf16[4,6,4096]{2,1,0:T(8,128)(2,1)} %reshape.136), calls=%async_computation.2 | async-start | bytes 524288 | tf_op jit(solution)/shard_map/all_to_all | solution.py:52
  314.2 0.9 fusion.19
  315.1 5.1 %all-to-all-done.1 = bf16[4,6,4096]{2,1,0:T(8,128)(2,1)S(1)} async-done(((bf16[4,6,4096]{2,1,0:T(8,128)(2,1)}), bf16[4,6,4096]{2,1,0:T(8,128)(2,1)S(1)}, u32[]{:S(2)}, u32[]{:S(2)}) %all-to-all-start.1) | async-done | bytes 196640 | tf_op jit(solution)/shard_map/all_to_all | solution.py:52
  320.2 0.9 fusion.18
  (40 shorter events, 0.3 us)
Async XLA Ops:
  7.2 1.9 copy-start
  7.2 13.1 %copy-start.5 = (s32[16,1]{0,1:T(1,128)S(1)}, s32[16,1]{0,1:T(1,128)}, u32[]{:S(2)}) copy-start(s32[16,1]{0,1:T(1,128)} %param.11) | copy-start | bytes 196
  7.2 13.6 %copy-start.3 = (bf16[16,4096]{1,0:T(8,128)(2,1)S(1)}, bf16[16,4096]{1,0:T(8,128)(2,1)}, u32[]{:S(2)}) copy-start(bf16[16,4096]{1,0:T(8,128)(2,1)} %param.10) | copy-start | bytes 393220
  7.2 57.7 %all-gather.6.cloned.1.call-start = ((), (), s32[]{:S(2)}) async-start(), calls=%async_computation.9 | async-start | bytes 1769472 | tf_op jit(solution)/shard_map/all_gather | solution.py:68
  9.3 21.1 %copy-start.4 = (bf16[16,4096]{1,0:T(8,128)(2,1)S(1)}, bf16[16,4096]{1,0:T(8,128)(2,1)}, u32[]{:S(2)}) copy-start(bf16[16,4096]{1,0:T(8,128)(2,1)} %param.12) | copy-start | bytes 393220
  20.3 90.0 %all-gather.4.cloned.1.call-start = ((), (), s32[]{:S(2)}) async-start(), calls=%async_computation.7 | async-start | bytes 1769472 | tf_op jit(solution)/shard_map/all_gather | solution.py:44
  21.0 43.9 %copy-start.8 = (bf16[1,192,1376]{2,1,0:T(8,128)(2,1)S(1)}, bf16[1,192,1376]{2,1,0:T(8,128)(2,1)}, u32[]{:S(2)}) copy-start(bf16[1,192,1376]{2,1,0:T(8,128)(2,1)} %param.16) | copy-start | bytes 1585156
  21.0 43.9 %copy-start.9 = (bf16[1,192,1376]{2,1,0:T(8,128)(2,1)S(1)}, bf16[1,192,1376]{2,1,0:T(8,128)(2,1)}, u32[]{:S(2)}) copy-start(bf16[1,192,1376]{2,1,0:T(8,128)(2,1)} %param.15) | copy-start | bytes 1585156
  30.4 124.8 %all-gather.8.cloned.1.call-start = ((), (), s32[]{:S(2)}) async-start(), calls=%async_computation.11 | async-start | bytes 1769472 | tf_op jit(solution)/shard_map/all_gather | solution.py:67
  39.9 192.0 %reduce-scatter.5.cloned.1.call-start = ((), (), s32[]{:S(2)}) async-start(), calls=%async_computation.10 | async-start | bytes 3538944 | tf_op jit(solution)/shard_map/reduce_scatter | solution.py:89
  64.9 15.2 %slice-start = ((s8[11272192]{0:T(1024)(128)(4,1)}), s8[4194304]{0:T(1024)(128)(4,1)S(1)}, s32[]{:S(2)}) async-start(s8[11272192]{0:T(1024)(128)(4,1)} %bitcast.79), calls=%async_computation.12 | async-start | bytes 8388608
  64.9 15.2 %slice-start.1 = ((s8[11272192]{0:T(1024)(128)(4,1)}), s8[2883584]{0:T(1024)(128)(4,1)S(1)}, s32[]{:S(2)}) async-start(s8[11272192]{0:T(1024)(128)(4,1)} %bitcast.79), calls=%async_computation.13 | async-start | bytes 5767168
  73.8 6.3 %copy-start.10 = (f32[192,1376]{1,0:T(8,128)}, f32[192,1376]{1,0:T(8,128)S(1)}, u32[]{:S(2)}) copy-start(f32[192,1376]{1,0:T(8,128)S(1)} %get-tuple-element.6) | copy-start | bytes 3170308
  73.9 6.3 %slice-start.2 = ((s8[11272192]{0:T(1024)(128)(4,1)}), s8[4194304]{0:T(1024)(128)(4,1)S(1)}, s32[]{:S(2)}) async-start(s8[11272192]{0:T(1024)(128)(4,1)} %bitcast.79), calls=%async_computation.14 | async-start | bytes 8388608
  84.6 224.4 %reduce-scatter.3.cloned.1.call-start = ((), (), s32[]{:S(2)}) async-start(), calls=%async_computation.8 | async-start | bytes 3538944 | tf_op jit(solution)/shard_map/reduce_scatter | solution.py:50
  110.3 9.7 %copy-start.7 = (bf16[192,4096]{1,0:T(8,128)(2,1)S(1)}, bf16[192,4096]{1,0:T(8,128)(2,1)}, u32[]{:S(2)}) copy-start(bf16[192,4096]{1,0:T(8,128)(2,1)} %all-gather.4.cloned.1.call-done) | copy-start | bytes 4718596
  135.9 1.6 copy-start.6
  155.1 82.0 %copy-start.2 = (bf16[192,4096]{1,0:T(8,128)(2,1)S(1)}, bf16[192,4096]{1,0:T(8,128)(2,1)}, u32[]{:S(2)}) copy-start(bf16[192,4096]{1,0:T(8,128)(2,1)} %all-gather.8.cloned.1.call-done) | copy-start | bytes 4718596
  233.7 77.1 %all-to-all-start.3 = ((bf16[4,6,4096]{2,1,0:T(8,128)(2,1)}), bf16[4,6,4096]{2,1,0:T(8,128)(2,1)S(1)}, u32[]{:S(2)}, u32[]{:S(2)}) async-start(bf16[4,6,4096]{2,1,0:T(8,128)(2,1)} %reshape.139), calls=%async_computation.5 | async-start | bytes 524288 | tf_op jit(solution)/shard_map/all_to_all | solution.py:91
  237.1 83.9 %copy-start.1 = (bf16[16,4096]{1,0:T(8,128)(2,1)S(1)}, bf16[16,4096]{1,0:T(8,128)(2,1)}, u32[]{:S(2)}) copy-start(bf16[16,4096]{1,0:T(8,128)(2,1)} %param.14) | copy-start | bytes 393220
  310.8 9.4 %all-to-all-start.1 = ((bf16[4,6,4096]{2,1,0:T(8,128)(2,1)}), bf16[4,6,4096]{2,1,0:T(8,128)(2,1)S(1)}, u32[]{:S(2)}, u32[]{:S(2)}) async-start(bf16[4,6,4096]{2,1,0:T(8,128)(2,1)} %reshape.136), calls=%async_computation.2 | async-start | bytes 524288 | tf_op jit(solution)/shard_map/all_to_all | solution.py:52
Sparse Core Ops, SparseCore 0:
  20.4 44.4 all-gather.5
  67.7 42.5 all-gather.3
  112.5 42.5 all-gather.7
  159.1 72.7 reduce-scatter.4
  235.3 73.6 reduce-scatter.2
where the time goes:
time: 328 us
  waiting for transfers between devices  199 us (61%)
  matrix products  70.1 us (21%)
  blocking collectives  27.1 us (8%)
  between operations  14 us (4%)
  starting transfers between devices  7.2 us (2%)
  local copies, waits for them, and re-layouts  5.84 us (2%)
  other arithmetic  4.02 us (1%)
    reduce_scatter x1, waiting for transfers between devices, backward_pass(): summed = lax.psum_scatter(terms, 'shard', scatter_dimension=0, tiled=True)  67.3 us
    reduce_scatter x1, waiting for transfers between devices, forward_pass(): summed = lax.psum_scatter(terms, 'shard', scatter_dimension=0, tiled=True)  65.8 us
    all_gather x1, waiting for transfers between devices, forward_pass(): piece = lax.all_gather(local_rows, 'shard', axis=0, tiled=True)  25.5 us
    all_gather x1, waiting for transfers between devices, backward_pass(): lax.all_gather(arrived_g.reshape(modes * CAP, width), 'shard', axis=0, ti...  25 us
    dot_general x3, matrix products, contract_last(): lax.dot_general(left, right, (((1,), (1,)), ((), ())), preferred_element_...  19.6 us
    dot_general x1, matrix products, forward_pass(): jnp.dot((jax.nn.silu(gate) * up).astype(jnp.bfloat16), down_w, preferred_...  15.8 us
    all_gather x1, waiting for transfers between devices, backward_pass(): lax.all_gather(arrived_x.reshape(modes * CAP, width), 'shard', axis=0, ti...  10.6 us
    all_to_all x1, blocking collectives, backward_pass(): lax.all_to_all(sent_g, 'mod', split_axis=0, concat_axis=0, tiled=True)  10.2 us
  transfers between devices with their start and end apart: 7, of which 6 were waited for; matrix products, arithmetic and copies ran while one was open for 23% of the time, Pallas kernels for 0%

commit v1 on v0

--- a/solution.py
+++ b/solution.py
@@ -41,7 +41,24 @@
     sent = dispatch(place, tokens_b, modes)
     arrived = lax.all_to_all(sent, "mod", split_axis=0, concat_axis=0, tiled=True)
     local_rows = arrived.reshape(modes * CAP, width)
-    piece = lax.all_gather(local_rows, "shard", axis=0, tiled=True)
+    size, mine, span = (lax.axis_size("shard"), lax.axis_index("shard"), local_rows.shape[0])
+    ahead = [(i, (i + 1) % size) for i in range(size)]
+    downward = [(i, (i - 1) % size) for i in range(size)]
+    out = jnp.zeros(
+        (*local_rows.shape[:0], size * span, *local_rows.shape[0 + 1 :]), local_rows.dtype
+    )
+    out = lax.dynamic_update_slice_in_dim(out, local_rows, mine * span, axis=0)
+    from_left = from_right = local_rows
+    halfway = size // 2
+    for lap in range(1, halfway + 1):
+        from_left = lax.ppermute(from_left, "shard", ahead)
+        out = lax.dynamic_update_slice_in_dim(out, from_left, (mine - lap) % size * span, axis=0)
+        if lap < size - halfway:
+            from_right = lax.ppermute(from_right, "shard", downward)
+            out = lax.dynamic_update_slice_in_dim(
+                out, from_right, (mine + lap) % size * span, axis=0
+            )
+    piece = out
     gate = jnp.dot(piece, gate_w, preferred_element_type=jnp.float32)
     up = jnp.dot(piece, up_w, preferred_element_type=jnp.float32)
     terms = jnp.dot(

time: 328 us -> 301 us (0.918)
  waiting for transfers between devices: 199 us -> 163 us
  starting transfers between devices: 7.2 us -> 31.5 us
  blocking collectives: 27.1 us -> 10 us
    ppermute x0 -> x7, waiting for transfers between devices: none -> 28.3 us  [the longest x4 28.3 us: forward_pass(): from_left = lax.ppermute(from_left, 'shard', ahead)]
    all_gather x1 -> x0, waiting for transfers between devices: 25.5 us -> none  [forward_pass(): piece = lax.all_gather(local_rows, 'shard', axis=0, tiled=True)]
    all_gather x1, waiting for transfers between devices: 25 us -> 0.02 us  [backward_pass(): lax.all_gather(arrived_g.reshape(modes * CAP, width), 'shard', axis=0, ti...]
    ppermute x0 -> x7, starting transfers between devices: none -> 17.5 us  [the longest x3 9.42 us: forward_pass(): from_right = lax.ppermute(from_right, 'shard', downward)]
    all_to_all x2 -> x0, blocking collectives: 16.9 us -> none  [the longest x1 8.52 us: forward_pass(): lax.all_to_all(sent, 'mod', split_axis=0, concat_axis=0, tiled=True)]
    all_gather x1, waiting for transfers between devices: 10.6 us -> 0.01 us  [backward_pass(): lax.all_gather(arrived_x.reshape(modes * CAP, width), 'shard', axis=0, ti...]
    reduce_scatter x1, waiting for transfers between devices: 65.8 us -> 58.2 us  [forward_pass(): summed = lax.psum_scatter(terms, 'shard', scatter_dimension=0, tiled=True)]
    all_to_all x0 -> x2, starting transfers between devices: none -> 6.81 us  [the longest x1 3.41 us: backward_pass(): lax.all_to_all(sent_x, 'mod', split_axis=0, concat_axis=0, tiled=True)]
  transfers between devices with their start and end apart: 7 -> 15, of which waited for: 6 -> 9; matrix products, arithmetic and copies ran while one was open for 23% -> 25% of each run, Pallas kernels for 0% -> 0%
where the time goes in v1:
time: 301 us; the launch traced here: 300 us
  waiting for transfers between devices  163 us (54%)
  matrix products  69.8 us (23%)
  starting transfers between devices  31.5 us (10%)
  between operations  14.2 us (5%)
  blocking collectives  10 us (3%)
  local copies, waits for them, and re-layouts  7.64 us (3%)
  other arithmetic  4.02 us (1%)
    reduce_scatter x1, waiting for transfers between devices, backward_pass(): summed = lax.psum_scatter(terms, 'shard', scatter_dimension=0, tiled=True)  65.6 us
    reduce_scatter x1, waiting for transfers between devices, forward_pass(): summed = lax.psum_scatter(terms, 'shard', scatter_dimension=0, tiled=True)  58.2 us
    ppermute x4, waiting for transfers between devices, forward_pass(): from_left = lax.ppermute(from_left, 'shard', ahead)  28.3 us
    dot_general x3, matrix products, contract_last(): lax.dot_general(left, right, (((1,), (1,)), ((), ())), preferred_element_...  19.7 us
    dot_general x1, matrix products, forward_pass(): jnp.dot((jax.nn.silu(gate) * up).astype(jnp.bfloat16), down_w, preferred_...  15.9 us
    all_to_all x1, blocking collectives, backward_pass(): lax.all_to_all(sent_g, 'mod', split_axis=0, concat_axis=0, tiled=True)  10 us
    dot_general x1, matrix products, backward_pass(): lax.dot_general(all_x, dup, outer, preferred_element_type=jnp.float32)  9.56 us
    ppermute x3, starting transfers between devices, forward_pass(): from_right = lax.ppermute(from_right, 'shard', downward)  9.42 us
  transfers between devices with their start and end apart: 15, of which 9 were waited for; matrix products, arithmetic and copies ran while one was open for 25% of the time, Pallas kernels for 0%

profile of v1, /device:TPU:0, one launch (start us, length us, event | category | flops | bytes accessed | tf_op | source)
XLA Modules:
  0.0 300.2 jit_solution(13085867982164877845)
XLA Ops:
  7.2 0.8 fusion.35
  8.2 0.8 select_reduce_fusion
  9.0 0.2 convolution_convert_fusion.4
  9.3 10.0 %all_to_all.25 = bf16[4,6,4096]{2,1,0:T(8,128)(2,1)S(1)} all-to-all(bf16[4,6,4096]{2,1,0:T(8,128)(2,1)S(1)} %reshape.137), channel_id=1, replica_groups=mesh['mod'=4,'shard'=8] {'mod'}, dimensions={0} | all-to-all | bytes 393216 | tf_op jit(solution)/shard_map/all_to_all | solution.py:81
  19.4 0.8 reshape.138
  20.4 0.2 select_reduce_fusion.1
  20.6 0.2 convolution_convert_fusion.5
  20.8 0.8 reshape.134
  21.6 3.4 %all-to-all-start = ((bf16[4,6,4096]{2,1,0:T(8,128)(2,1)}), bf16[4,6,4096]{2,1,0:T(8,128)(2,1)S(1)}, u32[]{:S(2)}, u32[]{:S(2)}) async-start(bf16[4,6,4096]{2,1,0:T(8,128)(2,1)} %reshape.134), calls=%async_computation | async-start | bytes 524288 | tf_op jit(solution)/shard_map/all_to_all | solution.py:42
  25.1 0.2 convolution_convert_fusion.3
  25.3 0.8 reshape.140
  26.1 4.9 %all-to-all-done = bf16[4,6,4096]{2,1,0:T(8,128)(2,1)S(1)} async-done(((bf16[4,6,4096]{2,1,0:T(8,128)(2,1)}), bf16[4,6,4096]{2,1,0:T(8,128)(2,1)S(1)}, u32[]{:S(2)}, u32[]{:S(2)}) %all-to-all-start) | async-done | bytes 196640 | tf_op jit(solution)/shard_map/all_to_all | solution.py:42
  30.9 3.4 %all-to-all-start.4 = ((bf16[4,6,4096]{2,1,0:T(8,128)(2,1)}), bf16[4,6,4096]{2,1,0:T(8,128)(2,1)S(1)}, u32[]{:S(2)}, u32[]{:S(2)}) async-start(bf16[4,6,4096]{2,1,0:T(8,128)(2,1)} %reshape.140), calls=%async_computation.6 | async-start | bytes 524288 | tf_op jit(solution)/shard_map/all_to_all | solution.py:80
  34.5 1.6 collective-permute-start
  36.1 3.2 %collective-permute-start.1 = (bf16[24,4096]{1,0:T(8,128)(2,1)S(1)}, bf16[24,4096]{1,0:T(8,128)(2,1)S(1)}, u32[]{:S(2)}, u32[]{:S(2)}) collective-permute-start(bf16[24,4096]{1,0:T(8,128)(2,1)S(1)} %reshape.135), channel_id=1, source_target_pairs={{0,7},{1,0},{2,1},{3,2},{4,3},{5,4},{6,5},{7,6},{8,15},{9,8},{10,9... | collective-permute-start | bytes 589832 | tf_op jit(solution)/shard_map/ppermute | solution.py:57
  39.5 0.9 all-to-all-done.4
  40.3 0.7 reshape.141
  41.2 4.7 %collective-permute-done = bf16[24,4096]{1,0:T(8,128)(2,1)S(1)} collective-permute-done((bf16[24,4096]{1,0:T(8,128)(2,1)S(1)}, bf16[24,4096]{1,0:T(8,128)(2,1)S(1)}, u32[]{:S(2)}, u32[]{:S(2)}) %collective-permute-start) | collective-permute-done | bytes 196640 | tf_op jit(solution)/shard_map/ppermute | solution.py:54
  45.9 1.6 collective-permute-start.2
  47.5 3.1 %collective-permute-start.3 = (bf16[24,4096]{1,0:T(8,128)(2,1)S(1)}, bf16[24,4096]{1,0:T(8,128)(2,1)S(1)}, u32[]{:S(2)}, u32[]{:S(2)}) collective-permute-start(bf16[24,4096]{1,0:T(8,128)(2,1)S(1)} %collective-permute-done.1), channel_id=1, source_target_pairs={{0,7},{1,0},{2,1},{3,2},{4,3},{5,4},{6,5},{7,6},{8,15},{9,8},{10,9... | collective-permute-start | bytes 589832 | tf_op jit(solution)/shard_map/ppermute | solution.py:57
  50.7 10.0 %collective-permute-done.2 = bf16[24,4096]{1,0:T(8,128)(2,1)S(1)} collective-permute-done((bf16[24,4096]{1,0:T(8,128)(2,1)S(1)}, bf16[24,4096]{1,0:T(8,128)(2,1)S(1)}, u32[]{:S(2)}, u32[]{:S(2)}) %collective-permute-start.2) | collective-permute-done | bytes 196640 | tf_op jit(solution)/shard_map/ppermute | solution.py:54
  60.6 2.5 collective-permute-start.4
  63.1 3.1 %collective-permute-start.5 = (bf16[24,4096]{1,0:T(8,128)(2,1)S(1)}, bf16[24,4096]{1,0:T(8,128)(2,1)S(1)}, u32[]{:S(2)}, u32[]{:S(2)}) collective-permute-start(bf16[24,4096]{1,0:T(8,128)(2,1)S(1)} %collective-permute-done.3), channel_id=1, source_target_pairs={{0,7},{1,0},{2,1},{3,2},{4,3},{5,4},{6,5},{7,6},{8,15},{9,8},{10,9... | collective-permute-start | bytes 589832 | tf_op jit(solution)/shard_map/ppermute | solution.py:57
  66.3 6.2 %collective-permute-done.4 = bf16[24,4096]{1,0:T(8,128)(2,1)S(1)} collective-permute-done((bf16[24,4096]{1,0:T(8,128)(2,1)S(1)}, bf16[24,4096]{1,0:T(8,128)(2,1)S(1)}, u32[]{:S(2)}, u32[]{:S(2)}) %collective-permute-start.4) | collective-permute-done | bytes 196640 | tf_op jit(solution)/shard_map/ppermute | solution.py:54
  72.5 2.5 collective-permute-start.6
  75.0 7.4 %collective-permute-done.6 = bf16[24,4096]{1,0:T(8,128)(2,1)S(1)} collective-permute-done((bf16[24,4096]{1,0:T(8,128)(2,1)S(1)}, bf16[24,4096]{1,0:T(8,128)(2,1)S(1)}, u32[]{:S(2)}, u32[]{:S(2)}) %collective-permute-start.6) | collective-permute-done | bytes 196640 | tf_op jit(solution)/shard_map/ppermute | solution.py:54
  82.4 9.1 %fusion.9 = f32[192,1376]{1,0:T(8,128)} fusion(bf16[192,4096]{1,0:T(8,128)(2,1)S(1)} %constant_dynamic-update-slice_fusion, bf16[1,4096,1376]{1,2,0:T(8,128)(2,1)} %param.18), kind=kOutput, calls=%fused_computation.12 | convolution fusion | flops 2164260864 | bytes 13901824 | tf_op jit(solution)/shard_map/dot_general | solution.py:63
  91.5 15.9 %fusion.5 = f32[192,4096]{1,0:T(8,128)} fusion(bf16[1,1376,4096]{2,1,0:T(8,128)(2,1)} %param.19, f32[192,1376]{1,0:T(8,128)} %fusion.9, bf16[192,4096]{1,0:T(8,128)(2,1)S(1)} %constant_dynamic-update-slice_fusion, bf16[1,4096,1376]{1,2,0:T(8,128)(2,1)} %param.17), kind=kOutput, calls=%fused_computation.8 | convolution fusion | flops 4330106880 | bytes 28319744 | tf_op jit(solution)/shard_map/dot_general | solution.py:64
  107.5 0.2 reduce-scatter.5.cloned.1.call-start
  107.7 0.8 copy-done.7
  108.7 9.1 %fusion.22 = (bf16[192,1376]{1,0:T(8,128)(2,1)S(1)}, f32[192,1376]{1,0:T(8,128)S(1)}) fusion(bf16[1,192,1376]{2,1,0:T(8,128)(2,1)S(1)} %copy-done.7, bf16[1,192,1376]{2,1,0:T(8,128)(2,1)S(1)} %copy-done.8, bf16[192,4096]{1,0:T(8,128)(2,1)} %all-gather.3.cloned.1.call-done, bf16[1,1376,4096]{2,1,0:T(8,128)(2,1)} %param.19), kind=kOutput, calls=%fused_computation.33 | convolution fusion | flops 2167431168 | bytes 15486976 | tf_op jit(solution)/shard_map/dot_general | solution.py:32
  117.8 6.2 %fusion.7 = f32[192,4096]{1,0:T(8,128)S(1)} fusion(bf16[1,4096,1376]{1,2,0:T(8,128)(2,1)} %param.18, f32[192,1376]{1,0:T(8,128)S(1)} %get-tuple-element.6, bf16[1,192,1376]{2,1,0:T(8,128)(2,1)S(1)} %copy-done.8), kind=kOutput, calls=%fused_computation.10 | convolution fusion | flops 2166110208 | bytes 16003072 | tf_op jit(solution)/shard_map/dot_general | solution.py:32
  124.1 4.4 %fusion.15 = f32[192,4096]{1,0:T(8,128)} fusion(f32[192,4096]{1,0:T(8,128)S(1)} %fusion.7, bf16[192,1376]{1,0:T(8,128)(2,1)S(1)} %get-tuple-element.5, bf16[1,4096,1376]{1,2,0:T(8,128)(2,1)S(1)} %bitcast.78), kind=kOutput, calls=%fused_computation.18 | convolution fusion | flops 2165047296 | bytes 18092032 | tf_op jit(solution)/shard_map/dot_general | solution.py:32
  128.5 1.4 copy-done.6
  129.9 7.1 %fusion = bf16[1,1376,4096]{2,1,0:T(8,128)(2,1)} fusion(bf16[192,4096]{1,0:T(8,128)(2,1)S(1)} %copy-done.6, bf16[1,192,1376]{2,1,0:T(8,128)(2,1)S(1)} %copy-done.7, bf16[1,192,1376]{2,1,0:T(8,128)(2,1)} %param.15), kind=kOutput, calls=%fused_computation.3 | convolution fusion | flops 2172010496 | bytes 13901824 | tf_op jit(solution)/shard_map/dot_general | solution.py:96
  137.0 9.6 %fusion.2 = bf16[1,4096,1376]{1,2,0:T(8,128)(2,1)} fusion(bf16[192,4096]{1,0:T(8,128)(2,1)} %all-gather.5.cloned.1.call-done, f32[192,1376]{1,0:T(8,128)} %copy-done.9, bf16[1,192,1376]{2,1,0:T(8,128)(2,1)} %param.15), kind=kOutput, calls=%fused_computation.5 | convolution fusion | flops 2171746304 | bytes 14430208 | tf_op jit(solution)/shard_map/dot_general | solution.py:102
  146.6 58.2 %reduce-scatter.3.cloned.1.call-done = f32[24,4096]{1,0:T(8,128)} async-done(((f32[192,4096]{1,0:T(8,128)}), f32[24,4096]{1,0:T(8,128)}) %reduce-scatter.3.cloned.1.call-update) | async-done | bytes 393232 | tf_op jit(solution)/shard_map/reduce_scatter | solution.py:67
  204.8 1.0 convert_element_type.102
  205.8 0.8 reshape.136
  206.6 3.4 %all-to-all-start.1 = ((bf16[4,6,4096]{2,1,0:T(8,128)(2,1)}), bf16[4,6,4096]{2,1,0:T(8,128)(2,1)S(1)}, u32[]{:S(2)}, u32[]{:S(2)}) async-start(bf16[4,6,4096]{2,1,0:T(8,128)(2,1)} %reshape.136), calls=%async_computation.2 | async-start | bytes 524288 | tf_op jit(solution)/shard_map/all_to_all | solution.py:69
  210.0 6.0 %fusion.1 = bf16[1,4096,1376]{1,2,0:T(8,128)(2,1)} fusion(bf16[192,4096]{1,0:T(8,128)(2,1)S(1)} %copy-done.2, bf16[192,1376]{1,0:T(8,128)(2,1)S(1)} %get-tuple-element.5), kind=kOutput, calls=%fused_computation.4 | convolution fusion | flops 2169896960 | bytes 13373440 | tf_op jit(solution)/shard_map/dot_general | solution.py:99
  216.0 65.6 %reduce-scatter.5.cloned.1.call-done = f32[24,4096]{1,0:T(8,128)} async-done(((f32[192,4096]{1,0:T(8,128)}), f32[24,4096]{1,0:T(8,128)}) %reduce-scatter.5.cloned.1.call-update) | async-done | bytes 393232 | tf_op jit(solution)/shard_map/reduce_scatter | solution.py:106
  281.6 1.0 convert_element_type.115
  282.6 0.8 reshape.139
  283.4 3.4 %all-to-all-start.3 = ((bf16[4,6,4096]{2,1,0:T(8,128)(2,1)}), bf16[4,6,4096]{2,1,0:T(8,128)(2,1)S(1)}, u32[]{:S(2)}, u32[]{:S(2)}) async-start(bf16[4,6,4096]{2,1,0:T(8,128)(2,1)} %reshape.139), calls=%async_computation.5 | async-start | bytes 524288 | tf_op jit(solution)/shard_map/all_to_all | solution.py:108
  286.8 0.9 fusion.18
  287.7 5.1 %all-to-all-done.3 = bf16[4,6,4096]{2,1,0:T(8,128)(2,1)S(1)} async-done(((bf16[4,6,4096]{2,1,0:T(8,128)(2,1)}), bf16[4,6,4096]{2,1,0:T(8,128)(2,1)S(1)}, u32[]{:S(2)}, u32[]{:S(2)}) %all-to-all-start.3) | async-done | bytes 196640 | tf_op jit(solution)/shard_map/all_to_all | solution.py:108
  292.8 0.9 fusion.19
  (60 shorter events, 1.3 us)
Async XLA Ops:
  7.2 1.9 copy-start
  7.2 13.0 %copy-start.5 = (s32[16,1]{0,1:T(1,128)S(1)}, s32[16,1]{0,1:T(1,128)}, u32[]{:S(2)}) copy-start(s32[16,1]{0,1:T(1,128)} %param.11) | copy-start | bytes 196
  7.2 13.4 %copy-start.3 = (bf16[16,4096]{1,0:T(8,128)(2,1)S(1)}, bf16[16,4096]{1,0:T(8,128)(2,1)}, u32[]{:S(2)}) copy-start(bf16[16,4096]{1,0:T(8,128)(2,1)} %param.10) | copy-start | bytes 393220
  7.2 100.5 %all-gather.3.cloned.1.call-start = ((), (), s32[]{:S(2)}) async-start(), calls=%async_computation.8 | async-start | bytes 1769472 | tf_op jit(solution)/shard_map/all_gather | solution.py:85
  9.2 15.9 %copy-start.4 = (bf16[16,4096]{1,0:T(8,128)(2,1)S(1)}, bf16[16,4096]{1,0:T(8,128)(2,1)}, u32[]{:S(2)}) copy-start(bf16[16,4096]{1,0:T(8,128)(2,1)} %param.12) | copy-start | bytes 393220
  21.6 9.4 %all-to-all-start = ((bf16[4,6,4096]{2,1,0:T(8,128)(2,1)}), bf16[4,6,4096]{2,1,0:T(8,128)(2,1)S(1)}, u32[]{:S(2)}, u32[]{:S(2)}) async-start(bf16[4,6,4096]{2,1,0:T(8,128)(2,1)} %reshape.134), calls=%async_computation | async-start | bytes 524288 | tf_op jit(solution)/shard_map/all_to_all | solution.py:42
  30.9 9.4 %all-to-all-start.4 = ((bf16[4,6,4096]{2,1,0:T(8,128)(2,1)}), bf16[4,6,4096]{2,1,0:T(8,128)(2,1)S(1)}, u32[]{:S(2)}, u32[]{:S(2)}) async-start(bf16[4,6,4096]{2,1,0:T(8,128)(2,1)} %reshape.140), calls=%async_computation.6 | async-start | bytes 524288 | tf_op jit(solution)/shard_map/all_to_all | solution.py:80
  34.4 102.6 %all-gather.5.cloned.1.call-start = ((), (), s32[]{:S(2)}) async-start(), calls=%async_computation.10 | async-start | bytes 1769472 | tf_op jit(solution)/shard_map/all_gather | solution.py:84
  34.5 11.4 %collective-permute-start = (bf16[24,4096]{1,0:T(8,128)(2,1)S(1)}, bf16[24,4096]{1,0:T(8,128)(2,1)S(1)}, u32[]{:S(2)}, u32[]{:S(2)}) collective-permute-start(bf16[24,4096]{1,0:T(8,128)(2,1)S(1)} %reshape.135), channel_id=1, source_target_pairs={{0,1},{1,2},{2,3},{3,4},{4,5},{5,6},{6,7},{7,0},{8,9},{9,10},{10,1... | collective-permute-start | bytes 589832 | tf_op jit(solution)/shard_map/ppermute | solution.py:54
  36.1 11.4 %collective-permute-start.1 = (bf16[24,4096]{1,0:T(8,128)(2,1)S(1)}, bf16[24,4096]{1,0:T(8,128)(2,1)S(1)}, u32[]{:S(2)}, u32[]{:S(2)}) collective-permute-start(bf16[24,4096]{1,0:T(8,128)(2,1)S(1)} %reshape.135), channel_id=1, source_target_pairs={{0,7},{1,0},{2,1},{3,2},{4,3},{5,4},{6,5},{7,6},{8,15},{9,8},{10,9... | collective-permute-start | bytes 589832 | tf_op jit(solution)/shard_map/ppermute | solution.py:57
  41.1 163.7 %reduce-scatter.3.cloned.1.call-start = ((), (), s32[]{:S(2)}) async-start(), calls=%async_computation.7 | async-start | bytes 3538944 | tf_op jit(solution)/shard_map/reduce_scatter | solution.py:67
  45.9 14.7 %collective-permute-start.2 = (bf16[24,4096]{1,0:T(8,128)(2,1)S(1)}, bf16[24,4096]{1,0:T(8,128)(2,1)S(1)}, u32[]{:S(2)}, u32[]{:S(2)}) collective-permute-start(bf16[24,4096]{1,0:T(8,128)(2,1)S(1)} %collective-permute-done), channel_id=1, source_target_pairs={{0,1},{1,2},{2,3},{3,4},{4,5},{5,6},{6,7},{7,0},{8,9},{9,10},{10,1... | collective-permute-start | bytes 589832 | tf_op jit(solution)/shard_map/ppermute | solution.py:54
  47.5 15.6 %collective-permute-start.3 = (bf16[24,4096]{1,0:T(8,128)(2,1)S(1)}, bf16[24,4096]{1,0:T(8,128)(2,1)S(1)}, u32[]{:S(2)}, u32[]{:S(2)}) collective-permute-start(bf16[24,4096]{1,0:T(8,128)(2,1)S(1)} %collective-permute-done.1), channel_id=1, source_target_pairs={{0,7},{1,0},{2,1},{3,2},{4,3},{5,4},{6,5},{7,6},{8,15},{9,8},{10,9... | collective-permute-start | bytes 589832 | tf_op jit(solution)/shard_map/ppermute | solution.py:57
  60.6 11.8 %collective-permute-start.4 = (bf16[24,4096]{1,0:T(8,128)(2,1)S(1)}, bf16[24,4096]{1,0:T(8,128)(2,1)S(1)}, u32[]{:S(2)}, u32[]{:S(2)}) collective-permute-start(bf16[24,4096]{1,0:T(8,128)(2,1)S(1)} %collective-permute-done.2), channel_id=1, source_target_pairs={{0,1},{1,2},{2,3},{3,4},{4,5},{5,6},{6,7},{7,0},{8,9},{9,10},{10,1... | collective-permute-start | bytes 589832 | tf_op jit(solution)/shard_map/ppermute | solution.py:54
  63.1 11.8 %collective-permute-start.5 = (bf16[24,4096]{1,0:T(8,128)(2,1)S(1)}, bf16[24,4096]{1,0:T(8,128)(2,1)S(1)}, u32[]{:S(2)}, u32[]{:S(2)}) collective-permute-start(bf16[24,4096]{1,0:T(8,128)(2,1)S(1)} %collective-permute-done.3), channel_id=1, source_target_pairs={{0,7},{1,0},{2,1},{3,2},{4,3},{5,4},{6,5},{7,6},{8,15},{9,8},{10,9... | collective-permute-start | bytes 589832 | tf_op jit(solution)/shard_map/ppermute | solution.py:57
  72.5 10.0 %collective-permute-start.6 = (bf16[24,4096]{1,0:T(8,128)(2,1)S(1)}, bf16[24,4096]{1,0:T(8,128)(2,1)S(1)}, u32[]{:S(2)}, u32[]{:S(2)}) collective-permute-start(bf16[24,4096]{1,0:T(8,128)(2,1)S(1)} %collective-permute-done.4), channel_id=1, source_target_pairs={{0,1},{1,2},{2,3},{3,4},{4,5},{5,6},{6,7},{7,0},{8,9},{9,10},{10,1... | collective-permute-start | bytes 589832 | tf_op jit(solution)/shard_map/ppermute | solution.py:54
  107.4 1.0 copy-start.7
  107.4 1.2 copy-start.8
  107.5 174.2 %reduce-scatter.5.cloned.1.call-start = ((), (), s32[]{:S(2)}) async-start(), calls=%async_computation.9 | async-start | bytes 3538944 | tf_op jit(solution)/shard_map/reduce_scatter | solution.py:106
  108.7 15.4 %slice-start = ((s8[11272192]{0:T(1024)(128)(4,1)}), s8[4194304]{0:T(1024)(128)(4,1)S(1)}, s32[]{:S(2)}) async-start(s8[11272192]{0:T(1024)(128)(4,1)} %bitcast.77), calls=%async_computation.11 | async-start | bytes 8388608
  108.7 15.4 %slice-start.1 = ((s8[11272192]{0:T(1024)(128)(4,1)}), s8[2883584]{0:T(1024)(128)(4,1)S(1)}, s32[]{:S(2)}) async-start(s8[11272192]{0:T(1024)(128)(4,1)} %bitcast.77), calls=%async_computation.12 | async-start | bytes 5767168
  117.7 6.3 %copy-start.9 = (f32[192,1376]{1,0:T(8,128)}, f32[192,1376]{1,0:T(8,128)S(1)}, u32[]{:S(2)}) copy-start(f32[192,1376]{1,0:T(8,128)S(1)} %get-tuple-element.6) | copy-start | bytes 3170308
  117.7 6.3 %slice-start.2 = ((s8[11272192]{0:T(1024)(128)(4,1)}), s8[4194304]{0:T(1024)(128)(4,1)S(1)}, s32[]{:S(2)}) async-start(s8[11272192]{0:T(1024)(128)(4,1)} %bitcast.77), calls=%async_computation.13 | async-start | bytes 8388608
  128.5 1.4 copy-start.6
  137.0 73.0 %copy-start.2 = (bf16[192,4096]{1,0:T(8,128)(2,1)S(1)}, bf16[192,4096]{1,0:T(8,128)(2,1)}, u32[]{:S(2)}) copy-start(bf16[192,4096]{1,0:T(8,128)(2,1)} %all-gather.5.cloned.1.call-done) | copy-start | bytes 4718596
  206.6 76.9 %all-to-all-start.1 = ((bf16[4,6,4096]{2,1,0:T(8,128)(2,1)}), bf16[4,6,4096]{2,1,0:T(8,128)(2,1)S(1)}, u32[]{:S(2)}, u32[]{:S(2)}) async-start(bf16[4,6,4096]{2,1,0:T(8,128)(2,1)} %reshape.136), calls=%async_computation.2 | async-start | bytes 524288 | tf_op jit(solution)/shard_map/all_to_all | solution.py:69
  210.0 83.7 %copy-start.1 = (bf16[16,4096]{1,0:T(8,128)(2,1)S(1)}, bf16[16,4096]{1,0:T(8,128)(2,1)}, u32[]{:S(2)}) copy-start(bf16[16,4096]{1,0:T(8,128)(2,1)} %param.14) | copy-start | bytes 393220
  283.4 9.4 %all-to-all-start.3 = ((bf16[4,6,4096]{2,1,0:T(8,128)(2,1)}), bf16[4,6,4096]{2,1,0:T(8,128)(2,1)S(1)}, u32[]{:S(2)}, u32[]{:S(2)}) async-start(bf16[4,6,4096]{2,1,0:T(8,128)(2,1)} %reshape.139), calls=%async_computation.5 | async-start | bytes 524288 | tf_op jit(solution)/shard_map/all_to_all | solution.py:108
Sparse Core Ops, SparseCore 0:
  20.3 57.7 all-gather.2
  80.9 47.0 all-gather.4
  132.1 72.6 reduce-scatter.2
  208.2 73.3 reduce-scatter.4
